TPU v7x, 32 devices: a whole 2x2x4 slice. The times are simulated.
32 devices in a mesh: depth: 8 (over z, x), rows: 4 (over y, core).
Axes of the slice: x: 2, y: 2, z: 4, core: 2. Of those that a mesh axis runs over, the one named last changes fastest.
Arguments:
- density: float32 [128, 64, 1024], P('depth', 'rows'), may hold values from 0 to 1
- bin_of_level: int32 [16], replicated, may hold values from 0 to 7
- absorb_bins: float32 [8], replicated, may hold values from 0.00234375 to 0.0625
- emit_bins: float32 [8], replicated, may hold values from 0.2 to 3
- occupancy: int32 [8, 4, 8], P('depth', 'rows'), may hold values 0 or 1
- col_offsets: int32 [1024], replicated, may hold values from 2 to 6
- row_offsets: int32 [64], P('rows'), may hold values from 2 to 6
Outputs:
- front_transmittance: float32 [8, 64, 1024], P('depth', 'rows')
- final_image: float32 [2, 64, 1024], P(None, 'rows')
All inputs are finite; a program needn't handle non-finite values. No bound on the sum of `occupancy` on one device may be relied on, other than what follows from the above.
Results may differ from a plain program's by a relative error of at most 0.0002.
Values sent between devices are 32-bit elements; how exact they have to be, the bound alone decides.
A program may use at most 64 MiB of HBM per device.

v0:
```python
import jax
import jax.numpy as jnp
from jax import lax
from jax.sharding import PartitionSpec as P


def from_behind(block, axis, distance):
    devices = range(lax.axis_size(axis))
    route = [(i - distance, i) for i in devices if i - distance in devices]
    return lax.ppermute(block, axis, route)


def resample_columns(mixed, col_offsets):
    fraction = col_offsets.astype(jnp.float32) / 8.0
    pad_shape = mixed.shape[:-1] + (1,)
    right_side = jnp.concatenate([mixed[..., 1:], jnp.zeros(pad_shape, jnp.float32)], -1)
    return (1.0 - fraction) * mixed + fraction * right_side


def tables(bin_of_level, absorb_bins, emit_bins):
    count_bins = absorb_bins.shape[0]
    onehot = (bin_of_level[:, None] == jnp.arange(count_bins, dtype=jnp.int32)[None, :]).astype(
        jnp.float32
    )
    return (jnp.sum(onehot * absorb_bins[None, :], 1), jnp.sum(onehot * emit_bins[None, :], 1))


def classify(sampled, absorb_level, emit_level):
    levels = absorb_level.shape[0]
    scaled = sampled * float(levels - 1)
    absorption = jnp.zeros(sampled.shape, jnp.float32)
    emission = jnp.zeros(sampled.shape, jnp.float32)
    for knot_index in range(levels):
        weight = jnp.maximum(0.0, 1.0 - jnp.abs(scaled - float(knot_index)))
        absorption = absorption + weight * absorb_level[knot_index]
        emission = emission + weight * emit_level[knot_index]
    return (absorption, emission)


def composite(absorption, emission):
    inclusive = jnp.cumsum(absorption, 0)
    exclusive = inclusive - absorption
    light = jnp.sum(jnp.exp(-exclusive) * (1.0 - jnp.exp(-absorption)) * emission, 0)
    return (light, inclusive[-1])


def on_device(density, bin_of_level, absorb_bins, emit_bins, occupancy, col_offsets, row_offsets):
    following = from_behind(density[:1], "depth", -1)
    extended = jnp.concatenate([density, following], 0)
    mid_depth = 0.5 * (extended[:-1] + extended[1:])
    row_below = from_behind(mid_depth[:, :1], "rows", -1)
    next_rows = jnp.concatenate([mid_depth[:, 1:], row_below], 1)
    frac_row = (row_offsets.astype(jnp.float32) / 8.0)[None, :, None]
    mixed = (1.0 - frac_row) * mid_depth + frac_row * next_rows
    sampled = resample_columns(mixed, col_offsets)
    absorb_level, emit_level = tables(bin_of_level, absorb_bins, emit_bins)
    occupied = occupancy[0, 0]
    absorption, emission = classify(sampled, absorb_level, emit_level)
    brick_mask = jnp.repeat(occupied.astype(jnp.float32), 128)
    absorption = absorption * brick_mask[None, None, :]
    light, depth_sum = composite(absorption, emission)
    position = lax.axis_index("depth")
    pieces = lax.all_gather(depth_sum[None], "depth", axis=0, tiled=True)
    shard_ids = jnp.arange(pieces.shape[0], dtype=jnp.int32)
    in_front = (shard_ids < position)[:, None, None]
    front_depth = jnp.sum(jnp.where(in_front, pieces, 0.0), 0)
    total_depth = jnp.sum(pieces, 0)
    front = jnp.exp(-front_depth)
    radiance = lax.psum(front * light, "depth")
    final_image = jnp.stack([radiance, jnp.exp(-total_depth)])
    return (front[None], final_image)


def solution(mesh):
    placed = (P("depth", "rows", None), P(), P(), P(), P("depth", "rows", None), P(), P("rows"))
    return jax.shard_map(
        on_device,
        mesh=mesh,
        in_specs=placed,
        out_specs=(P("depth", "rows", None), P(None, "rows", None)),
        check_vma=False,
    )
```

profile of v0, /device:TPU:0, one launch (start us, length us, event | category | flops | bytes accessed | tf_op | source)
XLA Modules:
  0.0 160.8 jit_solution(6802575559535258758)
XLA Ops:
  7.2 0.0 all-reduce.3.cloned.1.call-start
  7.2 0.8 slice.114
  8.1 0.0 copy-start.4
  8.1 1.4 collective-permute-start
  9.5 0.0 copy-done.2
  9.5 0.0 copy-done.3
  9.5 0.0 copy-done.4
  9.5 0.1 select_reduce_fusion.1
  9.6 0.0 copy-start.1
  9.6 0.7 fusion.59
  10.4 0.0 copy-done.5
  10.4 0.0 copy-done.1
  10.4 0.0 copy-start.6
  10.4 0.6 copy-done.6
  11.1 0.1 broadcast_bitcast_fusion
  11.1 0.7 fusion.58
  11.8 3.5 %collective-permute-done = f32[1,16,1024]{2,1,0:T(8,128)S(1)} collective-permute-done((f32[1,16,1024]{2,1,0:T(8,128)S(1)}, f32[1,16,1024]{2,1,0:T(8,128)S(1)}, u32[]{:S(2)}, u32[]{:S(2)}) %collective-permute-start) | collective-permute-done | bytes 65568 | tf_op jit(solution)/shard_map/ppermute | solution.py:10
  15.3 1.7 %fusion.3 = f32[16,16,1024]{2,1,0:T(8,128)S(1)} fusion(f32[16,16,1024]{2,1,0:T(8,128)} %param.7, f32[1,16,1024]{2,1,0:T(8,128)S(1)} %collective-permute-done), kind=kLoop, calls=%fused_computation.24 | loop fusion | flops 786432 | bytes 2162688 | tf_op jit(solution)/shard_map/mul | solution.py:50
  17.1 1.3 collective-permute-start.1
  18.4 0.0 copy-start
  18.4 0.1 slice.152
  18.6 1.7 %collective-permute-done.1 = f32[16,1,1024]{2,1,0:T(1,128)S(1)} collective-permute-done((f32[16,1,1024]{2,1,0:T(1,128)S(1)}, f32[16,1,1024]{2,1,0:T(1,128)S(1)}, u32[]{:S(2)}, u32[]{:S(2)}) %collective-permute-start.1) | collective-permute-done | bytes 65568 | tf_op jit(solution)/shard_map/ppermute | solution.py:10
  20.3 0.0 copy-done
  20.3 0.3 fusion.1
  20.6 0.3 slice.154
  21.0 28.9 %multiply_reduce_fusion = (f32[16,1024]{1,0:T(8,128)S(1)}, f32[16,16,1024]{2,1,0:T(8,128)S(1)}) fusion(f32[]{:T(128)} %bitcast.34, f32[]{:T(128)} %bitcast.33, f32[]{:T(128)} %bitcast.32, f32[]{:T(128)} %bitcast.31, f32[]{:T(128)} %bitcast.30, f32[]{:T(128)} %bitcast.29, f32[]{:T(128)} %bitcast.28, f32[]{:T(128)} %bitcast.27, f32[]{:T(128)} %bitcast.26, ...), kind=kOutput, calls=%fused_computation.4 | output fusion | flops 65781760 | bytes 3222656 | tf_op jit(solution)/shard_map/jit(cumsum)/reduce_window_sum | solution.py:41
  49.8 32.2 %all_gather.3 = f32[8,16,1024]{2,1,0:T(8,128)S(1)} all-gather(f32[1,16,1024]{2,1,0:T(8,128)S(1)} %slice.155), channel_id=1, replica_groups=mesh['depth'=8,'rows'=4] {'depth'}, dimensions={0}, use_global_device_ids=true | all-gather | bytes 589824 | tf_op jit(solution)/shard_map/all_gather | solution.py:63
  82.0 0.1 fusion.57
  82.1 0.7 multiply_bitcast_fusion
  82.8 0.0 all-reduce.3.cloned.1.call-update
  82.8 69.7 %all-reduce.3.cloned.1.call-done = f32[1,16,1024]{2,1,0:T(8,128)} async-done(((f32[1,16,1024]{2,1,0:T(8,128)}), f32[1,16,1024]{2,1,0:T(8,128)}) %all-reduce.3.cloned.1.call-update) | async-done | bytes 65552 | tf_op jit(solution)/shard_map/psum | solution.py:69
  152.5 1.5 pad_maximum_fusion.1
  (10 shorter events, 0.1 us)
Async XLA Ops:
  7.2 145.3 %all-reduce.3.cloned.1.call-start = ((), (), s32[]{:S(2)}) async-start(), calls=%async_computation | async-start | bytes 131072 | tf_op jit(solution)/shard_map/psum | solution.py:69
  8.1 1.5 copy-start.2
  8.1 1.5 copy-start.3
  8.1 1.5 copy-start.4
  8.1 7.2 %collective-permute-start = (f32[1,16,1024]{2,1,0:T(8,128)S(1)}, f32[1,16,1024]{2,1,0:T(8,128)S(1)}, u32[]{:S(2)}, u32[]{:S(2)}) collective-permute-start(f32[1,16,1024]{2,1,0:T(8,128)S(1)} %slice.114), channel_id=1, source_target_pairs={{4,0},{8,4},{12,8},{16,12},{20,16},{24,20},{28,24},{5,1},{9,5},{13... | collective-permute-start | bytes 196616 | tf_op jit(solution)/shard_map/ppermute | solution.py:10
  9.6 0.7 copy-start.5
  9.6 0.8 copy-start.1
  10.4 0.7 copy-start.6
  17.1 3.1 %collective-permute-start.1 = (f32[16,1,1024]{2,1,0:T(1,128)S(1)}, f32[16,1,1024]{2,1,0:T(1,128)S(1)}, u32[]{:S(2)}, u32[]{:S(2)}) collective-permute-start(f32[16,1,1024]{2,1,0:T(1,128)S(1)} %slice.153), channel_id=1, source_target_pairs={{1,0},{2,1},{3,2},{5,4},{6,5},{7,6},{9,8},{10,9},{11,10},{13,12},{... | collective-permute-start | bytes 196616 | tf_op jit(solution)/shard_map/ppermute | solution.py:10
  18.4 1.8 %copy-start = (f32[16,16,1024]{2,1,0:T(8,128)S(1)}, f32[16,16,1024]{2,1,0:T(8,128)}, u32[]{:S(2)}) copy-start(f32[16,16,1024]{2,1,0:T(8,128)} %param.7) | copy-start | bytes 3145732
Sparse Core Ops, SparseCore 0:
  82.9 69.5 all-reduce.2
where the time goes:
time: 161 us
  waiting for transfers between devices  74.8 us (46%)
  other arithmetic  33.3 us (21%)
  blocking collectives  32.2 us (20%)
  between operations  14.2 us (9%)
  local copies, waits for them, and re-layouts  3.52 us (2%)
  starting transfers between devices  2.75 us (2%)
    psum x1, waiting for transfers between devices, on_device(): radiance = lax.psum(front * light, 'depth')  69.7 us
    all_gather x1, blocking collectives, on_device(): pieces = lax.all_gather(depth_sum[None], 'depth', axis=0, tiled=True)  32.2 us
    another operation x1, other arithmetic, composite(): inclusive = jnp.cumsum(absorption, 0)  28.9 us
    ppermute x2, waiting for transfers between devices, from_behind(): return lax.ppermute(block, axis, route)  5.18 us
  transfers between devices with their start and end apart: 3, of which 3 were waited for; matrix products, arithmetic and copies ran while one was open for 1% of the time, Pallas kernels for 0%

commit v1 on v0

--- a/solution.py
+++ b/solution.py
@@ -60,7 +60,9 @@
     absorption = absorption * brick_mask[None, None, :]
     light, depth_sum = composite(absorption, emission)
     position = lax.axis_index("depth")
-    pieces = lax.all_gather(depth_sum[None], "depth", axis=0, tiled=True)
+    pieces = jnp.concatenate(
+        lax.all_to_all(jnp.stack([depth_sum[None]] * lax.axis_size("depth")), "depth", 0, 0), axis=0
+    )
     shard_ids = jnp.arange(pieces.shape[0], dtype=jnp.int32)
     in_front = (shard_ids < position)[:, None, None]
     front_depth = jnp.sum(jnp.where(in_front, pieces, 0.0), 0)

time: 161 us -> 151 us (0.938)
  blocking collectives: 32.2 us -> 0 us
  waiting for transfers between devices: 74.8 us -> 88.8 us
  starting transfers between devices: 2.75 us -> 8.82 us
    all_gather x1 -> x0, blocking collectives: 32.2 us -> none  [on_device(): pieces = lax.all_gather(depth_sum[None], 'depth', axis=0, tiled=True)]
    all_to_all x0 -> x1, waiting for transfers between devices: none -> 14.8 us  [on_device(): lax.all_to_all(jnp.stack([depth_sum[None]] * lax.axis_size('depth')), 'de...]
    all_to_all x0 -> x1, starting transfers between devices: none -> 6.21 us  [on_device(): lax.all_to_all(jnp.stack([depth_sum[None]] * lax.axis_size('depth')), 'de...]
  transfers between devices with their start and end apart: 3 -> 4, of which waited for: 3 -> 4; matrix products, arithmetic and copies ran while one was open for 1% -> 1% of each run, Pallas kernels for 0% -> 0%
where the time goes in v1:
time: 151 us; the launch traced here: 150 us
  waiting for transfers between devices  88.8 us (59%)
  other arithmetic  33.3 us (22%)
  between operations  14.2 us (9%)
  starting transfers between devices  8.82 us (6%)
  local copies, waits for them, and re-layouts  5.06 us (3%)
    psum x1, waiting for transfers between devices, on_device(): radiance = lax.psum(front * light, 'depth')  69.3 us
    another operation x1, other arithmetic, composite(): inclusive = jnp.cumsum(absorption, 0)  28.8 us
    all_to_all x1, waiting for transfers between devices, on_device(): lax.all_to_all(jnp.stack([depth_sum[None]] * lax.axis_size('depth')), 'de...  14.8 us
    all_to_all x1, starting transfers between devices, on_device(): lax.all_to_all(jnp.stack([depth_sum[None]] * lax.axis_size('depth')), 'de...  6.21 us
    ppermute x2, waiting for transfers between devices, from_behind(): return lax.ppermute(block, axis, route)  4.62 us
  transfers between devices with their start and end apart: 4, of which 4 were waited for; matrix products, arithmetic and copies ran while one was open for 1% of the time, Pallas kernels for 0%

profile of v1, /device:TPU:0, one launch (start us, length us, event | category | flops | bytes accessed | tf_op | source)
XLA Modules:
  0.0 150.2 jit_solution(3538832371163876174)
XLA Ops:
  7.2 0.0 copy-start.5
  7.2 0.0 copy-start.1
  7.2 0.9 slice.116
  8.0 1.3 collective-permute-start
  9.4 0.0 copy-start.6
  9.4 0.6 copy-done.6
  10.0 0.1 broadcast_bitcast_fusion
  10.1 0.6 copy-done.2
  10.7 0.0 copy-done.3
  10.7 0.0 copy-done.4
  10.7 0.1 select_reduce_fusion
  10.8 0.7 fusion.59
  11.5 3.6 %collective-permute-done = f32[1,16,1024]{2,1,0:T(8,128)S(1)} collective-permute-done((f32[1,16,1024]{2,1,0:T(8,128)S(1)}, f32[1,16,1024]{2,1,0:T(8,128)S(1)}, u32[]{:S(2)}, u32[]{:S(2)}) %collective-permute-start) | collective-permute-done | bytes 65568 | tf_op jit(solution)/shard_map/ppermute | solution.py:10
  15.1 1.7 %fusion.3 = f32[16,16,1024]{2,1,0:T(8,128)S(1)} fusion(f32[16,16,1024]{2,1,0:T(8,128)} %param.7, f32[1,16,1024]{2,1,0:T(8,128)S(1)} %collective-permute-done), kind=kLoop, calls=%fused_computation.24 | loop fusion | flops 786432 | bytes 2162688 | tf_op jit(solution)/shard_map/mul | solution.py:50
  16.9 1.3 collective-permute-start.1
  18.2 0.7 fusion.58
  19.0 0.0 copy-start
  19.0 0.1 slice.155
  19.1 1.0 collective-permute-done.1
  20.1 0.1 copy-done
  20.2 0.3 fusion.1
  20.5 0.3 slice.157
  20.9 28.8 %multiply_reduce_fusion = (f32[16,1024]{1,0:T(8,128)S(1)}, f32[16,16,1024]{2,1,0:T(8,128)S(1)}) fusion(f32[]{:T(128)} %bitcast.36, f32[]{:T(128)} %bitcast.35, f32[]{:T(128)} %bitcast.34, f32[]{:T(128)} %bitcast.33, f32[]{:T(128)} %bitcast.32, f32[]{:T(128)} %bitcast.31, f32[]{:T(128)} %bitcast.30, f32[]{:T(128)} %bitcast.29, f32[]{:T(128)} %bitcast.28, ...), kind=kOutput, calls=%fused_computation.4 | output fusion | flops 65781760 | bytes 3222656 | tf_op jit(solution)/shard_map/jit(cumsum)/reduce_window_sum | solution.py:41
  49.7 0.8 stack.10
  50.5 6.2 %all-to-all-start = ((f32[8,1,16,1024]{3,2,1,0:T(8,128)}), f32[8,1,16,1024]{3,2,1,0:T(8,128)S(1)}, u32[]{:S(2)}, u32[]{:S(2)}) async-start(f32[8,1,16,1024]{3,2,1,0:T(8,128)} %stack.10), calls=%async_computation | async-start | bytes 1048576 | tf_op jit(solution)/shard_map/all_to_all | solution.py:64
  56.7 0.0 all-reduce.3.cloned.1.call-start
  56.8 14.8 %all-to-all-done = f32[8,1,16,1024]{3,2,1,0:T(8,128)S(1)} async-done(((f32[8,1,16,1024]{3,2,1,0:T(8,128)}), f32[8,1,16,1024]{3,2,1,0:T(8,128)S(1)}, u32[]{:S(2)}, u32[]{:S(2)}) %all-to-all-start) | async-done | bytes 524320 | tf_op jit(solution)/shard_map/all_to_all | solution.py:64
  71.6 0.1 fusion.4
  71.8 0.7 multiply_bitcast_fusion
  72.4 0.0 all-reduce.3.cloned.1.call-update
  72.5 69.3 %all-reduce.3.cloned.1.call-done = f32[1,16,1024]{2,1,0:T(8,128)} async-done(((f32[1,16,1024]{2,1,0:T(8,128)}), f32[1,16,1024]{2,1,0:T(8,128)}) %all-reduce.3.cloned.1.call-update) | async-done | bytes 65552 | tf_op jit(solution)/shard_map/psum | solution.py:71
  141.8 1.5 %pad_maximum_fusion.1 = f32[2,16,1024]{2,1,0:T(8,128)} fusion(f32[1,16,1024]{2,1,0:T(8,128)S(1)} %exponential_bitcast_fusion, f32[1,16,1024]{2,1,0:T(8,128)} %all-reduce.3.cloned.1.call-done), kind=kLoop, calls=%fused_computation.61 | loop fusion | flops 32768 | bytes 262144 | tf_op jit(solution)/shard_map/stack | solution.py:72
  (13 shorter events, 0.1 us)
Async XLA Ops:
  7.2 2.2 %copy-start.5 = (s32[16]{0:T(128)S(1)}, s32[16]{0:T(128)}, u32[]{:S(2)}) copy-start(s32[16]{0:T(128)} %param.13) | copy-start | bytes 196
  7.2 2.2 %copy-start.1 = (s32[1024]{0:T(1024)S(1)}, s32[1024]{0:T(1024)}, u32[]{:S(2)}) copy-start(s32[1024]{0:T(1024)} %param.12) | copy-start | bytes 12292
  8.0 7.1 %collective-permute-start = (f32[1,16,1024]{2,1,0:T(8,128)S(1)}, f32[1,16,1024]{2,1,0:T(8,128)S(1)}, u32[]{:S(2)}, u32[]{:S(2)}) collective-permute-start(f32[1,16,1024]{2,1,0:T(8,128)S(1)} %slice.116), channel_id=1, source_target_pairs={{4,0},{8,4},{12,8},{16,12},{20,16},{24,20},{28,24},{5,1},{9,5},{13... | collective-permute-start | bytes 196616 | tf_op jit(solution)/shard_map/ppermute | solution.py:10
  9.4 0.7 copy-start.6
  10.0 0.7 copy-start.2
  10.0 0.7 copy-start.3
  10.0 0.7 copy-start.4
  16.9 3.1 %collective-permute-start.1 = (f32[16,1,1024]{2,1,0:T(1,128)S(1)}, f32[16,1,1024]{2,1,0:T(1,128)S(1)}, u32[]{:S(2)}, u32[]{:S(2)}) collective-permute-start(f32[16,1,1024]{2,1,0:T(1,128)S(1)} %slice.156), channel_id=1, source_target_pairs={{1,0},{2,1},{3,2},{5,4},{6,5},{7,6},{9,8},{10,9},{11,10},{13,12},{... | collective-permute-start | bytes 196616 | tf_op jit(solution)/shard_map/ppermute | solution.py:10
  19.0 1.2 copy-start
  50.5 21.1 %all-to-all-start = ((f32[8,1,16,1024]{3,2,1,0:T(8,128)}), f32[8,1,16,1024]{3,2,1,0:T(8,128)S(1)}, u32[]{:S(2)}, u32[]{:S(2)}) async-start(f32[8,1,16,1024]{3,2,1,0:T(8,128)} %stack.10), calls=%async_computation | async-start | bytes 1048576 | tf_op jit(solution)/shard_map/all_to_all | solution.py:64
  56.7 85.1 %all-reduce.3.cloned.1.call-start = ((), (), s32[]{:S(2)}) async-start(), calls=%async_computation.1 | async-start | bytes 131072 | tf_op jit(solution)/shard_map/psum | solution.py:71
Sparse Core Ops, SparseCore 0:
  72.6 69.2 all-reduce.2
